TPU v7x, 128 devices: a whole 4x4x4 slice. The times are simulated.
128 devices in a mesh: parts: 1, data: 128 (over z, y, x, core).
Axes of the slice: x: 4, y: 4, z: 4, core: 2. Of those that a mesh axis runs over, the one named last changes fastest.
Arguments:
- feat_rows: bfloat16 [1048576, 28], P('data')
- labels: int32 [1048576], P('data')
- pos_init: float32 [28, 64], P(None, 'parts')
- mom_init: float32 [28, 64], P(None, 'parts')
- step_sizes: float32 [64, 64], P(None, 'parts')
Outputs:
- output 1: float32 [28, 64], P(None, 'parts')
- output 2: float32 [28, 64], P(None, 'parts')
- output 3: float32 [64, 64], P(None, 'parts')
All inputs are finite; a program needn't handle non-finite values.
Results may differ from a plain program's by a relative error of at most 0.00335409.
Values are sent between devices in bfloat16 or wider.
A program may use at most 1 GiB of HBM per device.

v0:
```python
import jax
import jax.numpy as jnp
from jax import lax
from jax.sharding import PartitionSpec as P

PRIOR_VAR = 4.0


def solution(mesh):
    row_spec = P("data", None)
    chain_spec = P(None, "parts")

    def local_chains(feat_rows, labels, pos_init, mom_init, step_sizes):
        label_col = labels.astype(jnp.float32)[:, None]

        def gradient_at(positions):
            logits = jnp.dot(feat_rows, positions.astype(jnp.bfloat16), preferred_element_type=jnp.float32)
            residual = (label_col - jax.nn.sigmoid(logits)).astype(jnp.bfloat16)
            grad_part = lax.dot_general(feat_rows, residual, (((0,), (0,)), ((), ())), preferred_element_type=jnp.float32)
            gradient = lax.psum(grad_part, "data") - positions / PRIOR_VAR
            return gradient, logits

        grad_init, _ = gradient_at(pos_init)

        def leap_step(loop_state, step_size):
            positions, momentum, gradient = loop_state
            momentum = momentum + 0.5 * step_size * gradient
            positions = positions + step_size * momentum
            gradient, logits = gradient_at(positions)
            momentum = momentum + 0.5 * step_size * gradient
            loss_part = jnp.sum(jax.nn.softplus(logits) - label_col * logits, axis=0)
            potential = lax.psum(loss_part, "data") + jnp.sum(positions * positions, axis=0) / (2.0 * PRIOR_VAR)
            energy = potential + 0.5 * jnp.sum(momentum * momentum, axis=0)
            return (positions, momentum, gradient), energy

        (positions, momentum, _), energies = lax.scan(leap_step, (pos_init, mom_init, grad_init), step_sizes)
        return positions, momentum, energies

    return jax.shard_map(local_chains, mesh=mesh, in_specs=(row_spec, P("data"), chain_spec, chain_spec, chain_spec), out_specs=(chain_spec, chain_spec, chain_spec), check_vma=False)
```

profile of v0, /device:TPU:1, one launch (start us, length us, event | category | flops | bytes accessed | tf_op | source)
XLA Modules:
  0.0 4428.4 jit_solution(17588999508205589823)
XLA Ops:
  4.2 68.8 %psum.21 = f32[28,64]{1,0:T(8,128)S(1)} all-reduce(f32[28,64]{1,0:T(8,128)S(1)} %fusion.11), channel_id=1, replica_groups=mesh['parts'=1,'data'=128] {'data'}, use_global_device_ids=true, to_apply=%region_0.0 | all-reduce | flops 1792 | bytes 14336 | tf_op jit(solution)/shard_map/psum | solution.py:20
  73.0 4354.8 %while.16 = (s32[]{:T(128)}, f32[28,64]{1,0:T(8,128)S(1)}, f32[28,64]{1,0:T(8,128)S(1)}, f32[28,64]{1,0:T(8,128)S(1)}, f32[64,64]{1,0:T(8,128)}, /*index=5*/f32[...) while((s32[]{:T(128)}, f32[28,64]{1,0:T(8,128)S(1)}, ...), condition=%wide.region_7.8_spmd, body=%wide.region_1.7_spmd.sunk | while | flops 66089152 | bytes 5282157 | solution.py:36
  76.2 62.8 %all-reduce.2 = (f32[28,64]{1,0:T(8,128)S(1)}, f32[64]{0:T(128)S(1)}) all-reduce(f32[28,64]{1,0:T(8,128)S(1)} %convolution_bitcast_fusion.3, f32[64]{0:T(128)S(1)} %get-tuple-element.141), channel_id=1, replica_groups=mesh['parts'=1,'data'=128] {'data'}, use_global_device_ids=true, to_apply=%region_2.2 | all-reduce | flops 1856 | bytes 14848 | tf_op jit(solution)/shard_map/while/body/eval_jaxpr/psum | solution.py:20
  143.6 64.2 %all-reduce.2 = (f32[28,64]{1,0:T(8,128)S(1)}, f32[64]{0:T(128)S(1)}) all-reduce(f32[28,64]{1,0:T(8,128)S(1)} %convolution_bitcast_fusion.3, f32[64]{0:T(128)S(1)} %get-tuple-element.141), channel_id=1, replica_groups=mesh['parts'=1,'data'=128] {'data'}, use_global_device_ids=true, to_apply=%region_2.2 | all-reduce | flops 1856 | bytes 14848 | tf_op jit(solution)/shard_map/while/body/eval_jaxpr/psum | solution.py:20
  212.4 62.8 %all-reduce.2 = (f32[28,64]{1,0:T(8,128)S(1)}, f32[64]{0:T(128)S(1)}) all-reduce(f32[28,64]{1,0:T(8,128)S(1)} %convolution_bitcast_fusion.3, f32[64]{0:T(128)S(1)} %get-tuple-element.141), channel_id=1, replica_groups=mesh['parts'=1,'data'=128] {'data'}, use_global_device_ids=true, to_apply=%region_2.2 | all-reduce | flops 1856 | bytes 14848 | tf_op jit(solution)/shard_map/while/body/eval_jaxpr/psum | solution.py:20
  279.7 64.2 %all-reduce.2 = (f32[28,64]{1,0:T(8,128)S(1)}, f32[64]{0:T(128)S(1)}) all-reduce(f32[28,64]{1,0:T(8,128)S(1)} %convolution_bitcast_fusion.3, f32[64]{0:T(128)S(1)} %get-tuple-element.141), channel_id=1, replica_groups=mesh['parts'=1,'data'=128] {'data'}, use_global_device_ids=true, to_apply=%region_2.2 | all-reduce | flops 1856 | bytes 14848 | tf_op jit(solution)/shard_map/while/body/eval_jaxpr/psum | solution.py:20
  348.5 62.8 %all-reduce.2 = (f32[28,64]{1,0:T(8,128)S(1)}, f32[64]{0:T(128)S(1)}) all-reduce(f32[28,64]{1,0:T(8,128)S(1)} %convolution_bitcast_fusion.3, f32[64]{0:T(128)S(1)} %get-tuple-element.141), channel_id=1, replica_groups=mesh['parts'=1,'data'=128] {'data'}, use_global_device_ids=true, to_apply=%region_2.2 | all-reduce | flops 1856 | bytes 14848 | tf_op jit(solution)/shard_map/while/body/eval_jaxpr/psum | solution.py:20
  415.8 64.2 %all-reduce.2 = (f32[28,64]{1,0:T(8,128)S(1)}, f32[64]{0:T(128)S(1)}) all-reduce(f32[28,64]{1,0:T(8,128)S(1)} %convolution_bitcast_fusion.3, f32[64]{0:T(128)S(1)} %get-tuple-element.141), channel_id=1, replica_groups=mesh['parts'=1,'data'=128] {'data'}, use_global_device_ids=true, to_apply=%region_2.2 | all-reduce | flops 1856 | bytes 14848 | tf_op jit(solution)/shard_map/while/body/eval_jaxpr/psum | solution.py:20
  484.5 62.8 %all-reduce.2 = (f32[28,64]{1,0:T(8,128)S(1)}, f32[64]{0:T(128)S(1)}) all-reduce(f32[28,64]{1,0:T(8,128)S(1)} %convolution_bitcast_fusion.3, f32[64]{0:T(128)S(1)} %get-tuple-element.141), channel_id=1, replica_groups=mesh['parts'=1,'data'=128] {'data'}, use_global_device_ids=true, to_apply=%region_2.2 | all-reduce | flops 1856 | bytes 14848 | tf_op jit(solution)/shard_map/while/body/eval_jaxpr/psum | solution.py:20
  551.8 64.2 %all-reduce.2 = (f32[28,64]{1,0:T(8,128)S(1)}, f32[64]{0:T(128)S(1)}) all-reduce(f32[28,64]{1,0:T(8,128)S(1)} %convolution_bitcast_fusion.3, f32[64]{0:T(128)S(1)} %get-tuple-element.141), channel_id=1, replica_groups=mesh['parts'=1,'data'=128] {'data'}, use_global_device_ids=true, to_apply=%region_2.2 | all-reduce | flops 1856 | bytes 14848 | tf_op jit(solution)/shard_map/while/body/eval_jaxpr/psum | solution.py:20
  620.6 62.8 %all-reduce.2 = (f32[28,64]{1,0:T(8,128)S(1)}, f32[64]{0:T(128)S(1)}) all-reduce(f32[28,64]{1,0:T(8,128)S(1)} %convolution_bitcast_fusion.3, f32[64]{0:T(128)S(1)} %get-tuple-element.141), channel_id=1, replica_groups=mesh['parts'=1,'data'=128] {'data'}, use_global_device_ids=true, to_apply=%region_2.2 | all-reduce | flops 1856 | bytes 14848 | tf_op jit(solution)/shard_map/while/body/eval_jaxpr/psum | solution.py:20
  687.9 64.2 %all-reduce.2 = (f32[28,64]{1,0:T(8,128)S(1)}, f32[64]{0:T(128)S(1)}) all-reduce(f32[28,64]{1,0:T(8,128)S(1)} %convolution_bitcast_fusion.3, f32[64]{0:T(128)S(1)} %get-tuple-element.141), channel_id=1, replica_groups=mesh['parts'=1,'data'=128] {'data'}, use_global_device_ids=true, to_apply=%region_2.2 | all-reduce | flops 1856 | bytes 14848 | tf_op jit(solution)/shard_map/while/body/eval_jaxpr/psum | solution.py:20
  756.7 62.8 %all-reduce.2 = (f32[28,64]{1,0:T(8,128)S(1)}, f32[64]{0:T(128)S(1)}) all-reduce(f32[28,64]{1,0:T(8,128)S(1)} %convolution_bitcast_fusion.3, f32[64]{0:T(128)S(1)} %get-tuple-element.141), channel_id=1, replica_groups=mesh['parts'=1,'data'=128] {'data'}, use_global_device_ids=true, to_apply=%region_2.2 | all-reduce | flops 1856 | bytes 14848 | tf_op jit(solution)/shard_map/while/body/eval_jaxpr/psum | solution.py:20
  824.0 64.2 %all-reduce.2 = (f32[28,64]{1,0:T(8,128)S(1)}, f32[64]{0:T(128)S(1)}) all-reduce(f32[28,64]{1,0:T(8,128)S(1)} %convolution_bitcast_fusion.3, f32[64]{0:T(128)S(1)} %get-tuple-element.141), channel_id=1, replica_groups=mesh['parts'=1,'data'=128] {'data'}, use_global_device_ids=true, to_apply=%region_2.2 | all-reduce | flops 1856 | bytes 14848 | tf_op jit(solution)/shard_map/while/body/eval_jaxpr/psum | solution.py:20
  892.8 62.8 %all-reduce.2 = (f32[28,64]{1,0:T(8,128)S(1)}, f32[64]{0:T(128)S(1)}) all-reduce(f32[28,64]{1,0:T(8,128)S(1)} %convolution_bitcast_fusion.3, f32[64]{0:T(128)S(1)} %get-tuple-element.141), channel_id=1, replica_groups=mesh['parts'=1,'data'=128] {'data'}, use_global_device_ids=true, to_apply=%region_2.2 | all-reduce | flops 1856 | bytes 14848 | tf_op jit(solution)/shard_map/while/body/eval_jaxpr/psum | solution.py:20
  960.1 64.2 %all-reduce.2 = (f32[28,64]{1,0:T(8,128)S(1)}, f32[64]{0:T(128)S(1)}) all-reduce(f32[28,64]{1,0:T(8,128)S(1)} %convolution_bitcast_fusion.3, f32[64]{0:T(128)S(1)} %get-tuple-element.141), channel_id=1, replica_groups=mesh['parts'=1,'data'=128] {'data'}, use_global_device_ids=true, to_apply=%region_2.2 | all-reduce | flops 1856 | bytes 14848 | tf_op jit(solution)/shard_map/while/body/eval_jaxpr/psum | solution.py:20
  1028.9 62.8 %all-reduce.2 = (f32[28,64]{1,0:T(8,128)S(1)}, f32[64]{0:T(128)S(1)}) all-reduce(f32[28,64]{1,0:T(8,128)S(1)} %convolution_bitcast_fusion.3, f32[64]{0:T(128)S(1)} %get-tuple-element.141), channel_id=1, replica_groups=mesh['parts'=1,'data'=128] {'data'}, use_global_device_ids=true, to_apply=%region_2.2 | all-reduce | flops 1856 | bytes 14848 | tf_op jit(solution)/shard_map/while/body/eval_jaxpr/psum | solution.py:20
  1096.2 64.2 %all-reduce.2 = (f32[28,64]{1,0:T(8,128)S(1)}, f32[64]{0:T(128)S(1)}) all-reduce(f32[28,64]{1,0:T(8,128)S(1)} %convolution_bitcast_fusion.3, f32[64]{0:T(128)S(1)} %get-tuple-element.141), channel_id=1, replica_groups=mesh['parts'=1,'data'=128] {'data'}, use_global_device_ids=true, to_apply=%region_2.2 | all-reduce | flops 1856 | bytes 14848 | tf_op jit(solution)/shard_map/while/body/eval_jaxpr/psum | solution.py:20
  1165.0 62.8 %all-reduce.2 = (f32[28,64]{1,0:T(8,128)S(1)}, f32[64]{0:T(128)S(1)}) all-reduce(f32[28,64]{1,0:T(8,128)S(1)} %convolution_bitcast_fusion.3, f32[64]{0:T(128)S(1)} %get-tuple-element.141), channel_id=1, replica_groups=mesh['parts'=1,'data'=128] {'data'}, use_global_device_ids=true, to_apply=%region_2.2 | all-reduce | flops 1856 | bytes 14848 | tf_op jit(solution)/shard_map/while/body/eval_jaxpr/psum | solution.py:20
  1232.3 64.2 %all-reduce.2 = (f32[28,64]{1,0:T(8,128)S(1)}, f32[64]{0:T(128)S(1)}) all-reduce(f32[28,64]{1,0:T(8,128)S(1)} %convolution_bitcast_fusion.3, f32[64]{0:T(128)S(1)} %get-tuple-element.141), channel_id=1, replica_groups=mesh['parts'=1,'data'=128] {'data'}, use_global_device_ids=true, to_apply=%region_2.2 | all-reduce | flops 1856 | bytes 14848 | tf_op jit(solution)/shard_map/while/body/eval_jaxpr/psum | solution.py:20
  1301.0 62.8 %all-reduce.2 = (f32[28,64]{1,0:T(8,128)S(1)}, f32[64]{0:T(128)S(1)}) all-reduce(f32[28,64]{1,0:T(8,128)S(1)} %convolution_bitcast_fusion.3, f32[64]{0:T(128)S(1)} %get-tuple-element.141), channel_id=1, replica_groups=mesh['parts'=1,'data'=128] {'data'}, use_global_device_ids=true, to_apply=%region_2.2 | all-reduce | flops 1856 | bytes 14848 | tf_op jit(solution)/shard_map/while/body/eval_jaxpr/psum | solution.py:20
  1368.4 64.2 %all-reduce.2 = (f32[28,64]{1,0:T(8,128)S(1)}, f32[64]{0:T(128)S(1)}) all-reduce(f32[28,64]{1,0:T(8,128)S(1)} %convolution_bitcast_fusion.3, f32[64]{0:T(128)S(1)} %get-tuple-element.141), channel_id=1, replica_groups=mesh['parts'=1,'data'=128] {'data'}, use_global_device_ids=true, to_apply=%region_2.2 | all-reduce | flops 1856 | bytes 14848 | tf_op jit(solution)/shard_map/while/body/eval_jaxpr/psum | solution.py:20
  1437.1 62.8 %all-reduce.2 = (f32[28,64]{1,0:T(8,128)S(1)}, f32[64]{0:T(128)S(1)}) all-reduce(f32[28,64]{1,0:T(8,128)S(1)} %convolution_bitcast_fusion.3, f32[64]{0:T(128)S(1)} %get-tuple-element.141), channel_id=1, replica_groups=mesh['parts'=1,'data'=128] {'data'}, use_global_device_ids=true, to_apply=%region_2.2 | all-reduce | flops 1856 | bytes 14848 | tf_op jit(solution)/shard_map/while/body/eval_jaxpr/psum | solution.py:20
  1504.4 64.2 %all-reduce.2 = (f32[28,64]{1,0:T(8,128)S(1)}, f32[64]{0:T(128)S(1)}) all-reduce(f32[28,64]{1,0:T(8,128)S(1)} %convolution_bitcast_fusion.3, f32[64]{0:T(128)S(1)} %get-tuple-element.141), channel_id=1, replica_groups=mesh['parts'=1,'data'=128] {'data'}, use_global_device_ids=true, to_apply=%region_2.2 | all-reduce | flops 1856 | bytes 14848 | tf_op jit(solution)/shard_map/while/body/eval_jaxpr/psum | solution.py:20
  1573.2 62.8 %all-reduce.2 = (f32[28,64]{1,0:T(8,128)S(1)}, f32[64]{0:T(128)S(1)}) all-reduce(f32[28,64]{1,0:T(8,128)S(1)} %convolution_bitcast_fusion.3, f32[64]{0:T(128)S(1)} %get-tuple-element.141), channel_id=1, replica_groups=mesh['parts'=1,'data'=128] {'data'}, use_global_device_ids=true, to_apply=%region_2.2 | all-reduce | flops 1856 | bytes 14848 | tf_op jit(solution)/shard_map/while/body/eval_jaxpr/psum | solution.py:20
  1640.5 64.2 %all-reduce.2 = (f32[28,64]{1,0:T(8,128)S(1)}, f32[64]{0:T(128)S(1)}) all-reduce(f32[28,64]{1,0:T(8,128)S(1)} %convolution_bitcast_fusion.3, f32[64]{0:T(128)S(1)} %get-tuple-element.141), channel_id=1, replica_groups=mesh['parts'=1,'data'=128] {'data'}, use_global_device_ids=true, to_apply=%region_2.2 | all-reduce | flops 1856 | bytes 14848 | tf_op jit(solution)/shard_map/while/body/eval_jaxpr/psum | solution.py:20
  1709.3 62.8 %all-reduce.2 = (f32[28,64]{1,0:T(8,128)S(1)}, f32[64]{0:T(128)S(1)}) all-reduce(f32[28,64]{1,0:T(8,128)S(1)} %convolution_bitcast_fusion.3, f32[64]{0:T(128)S(1)} %get-tuple-element.141), channel_id=1, replica_groups=mesh['parts'=1,'data'=128] {'data'}, use_global_device_ids=true, to_apply=%region_2.2 | all-reduce | flops 1856 | bytes 14848 | tf_op jit(solution)/shard_map/while/body/eval_jaxpr/psum | solution.py:20
  1776.6 64.2 %all-reduce.2 = (f32[28,64]{1,0:T(8,128)S(1)}, f32[64]{0:T(128)S(1)}) all-reduce(f32[28,64]{1,0:T(8,128)S(1)} %convolution_bitcast_fusion.3, f32[64]{0:T(128)S(1)} %get-tuple-element.141), channel_id=1, replica_groups=mesh['parts'=1,'data'=128] {'data'}, use_global_device_ids=true, to_apply=%region_2.2 | all-reduce | flops 1856 | bytes 14848 | tf_op jit(solution)/shard_map/while/body/eval_jaxpr/psum | solution.py:20
  1845.4 62.8 %all-reduce.2 = (f32[28,64]{1,0:T(8,128)S(1)}, f32[64]{0:T(128)S(1)}) all-reduce(f32[28,64]{1,0:T(8,128)S(1)} %convolution_bitcast_fusion.3, f32[64]{0:T(128)S(1)} %get-tuple-element.141), channel_id=1, replica_groups=mesh['parts'=1,'data'=128] {'data'}, use_global_device_ids=true, to_apply=%region_2.2 | all-reduce | flops 1856 | bytes 14848 | tf_op jit(solution)/shard_map/while/body/eval_jaxpr/psum | solution.py:20
  1912.7 64.2 %all-reduce.2 = (f32[28,64]{1,0:T(8,128)S(1)}, f32[64]{0:T(128)S(1)}) all-reduce(f32[28,64]{1,0:T(8,128)S(1)} %convolution_bitcast_fusion.3, f32[64]{0:T(128)S(1)} %get-tuple-element.141), channel_id=1, replica_groups=mesh['parts'=1,'data'=128] {'data'}, use_global_device_ids=true, to_apply=%region_2.2 | all-reduce | flops 1856 | bytes 14848 | tf_op jit(solution)/shard_map/while/body/eval_jaxpr/psum | solution.py:20
  1981.5 62.8 %all-reduce.2 = (f32[28,64]{1,0:T(8,128)S(1)}, f32[64]{0:T(128)S(1)}) all-reduce(f32[28,64]{1,0:T(8,128)S(1)} %convolution_bitcast_fusion.3, f32[64]{0:T(128)S(1)} %get-tuple-element.141), channel_id=1, replica_groups=mesh['parts'=1,'data'=128] {'data'}, use_global_device_ids=true, to_apply=%region_2.2 | all-reduce | flops 1856 | bytes 14848 | tf_op jit(solution)/shard_map/while/body/eval_jaxpr/psum | solution.py:20
  2048.8 64.2 %all-reduce.2 = (f32[28,64]{1,0:T(8,128)S(1)}, f32[64]{0:T(128)S(1)}) all-reduce(f32[28,64]{1,0:T(8,128)S(1)} %convolution_bitcast_fusion.3, f32[64]{0:T(128)S(1)} %get-tuple-element.141), channel_id=1, replica_groups=mesh['parts'=1,'data'=128] {'data'}, use_global_device_ids=true, to_apply=%region_2.2 | all-reduce | flops 1856 | bytes 14848 | tf_op jit(solution)/shard_map/while/body/eval_jaxpr/psum | solution.py:20
  2117.5 62.8 %all-reduce.2 = (f32[28,64]{1,0:T(8,128)S(1)}, f32[64]{0:T(128)S(1)}) all-reduce(f32[28,64]{1,0:T(8,128)S(1)} %convolution_bitcast_fusion.3, f32[64]{0:T(128)S(1)} %get-tuple-element.141), channel_id=1, replica_groups=mesh['parts'=1,'data'=128] {'data'}, use_global_device_ids=true, to_apply=%region_2.2 | all-reduce | flops 1856 | bytes 14848 | tf_op jit(solution)/shard_map/while/body/eval_jaxpr/psum | solution.py:20
  2184.9 64.2 %all-reduce.2 = (f32[28,64]{1,0:T(8,128)S(1)}, f32[64]{0:T(128)S(1)}) all-reduce(f32[28,64]{1,0:T(8,128)S(1)} %convolution_bitcast_fusion.3, f32[64]{0:T(128)S(1)} %get-tuple-element.141), channel_id=1, replica_groups=mesh['parts'=1,'data'=128] {'data'}, use_global_device_ids=true, to_apply=%region_2.2 | all-reduce | flops 1856 | bytes 14848 | tf_op jit(solution)/shard_map/while/body/eval_jaxpr/psum | solution.py:20
  2253.6 62.8 %all-reduce.2 = (f32[28,64]{1,0:T(8,128)S(1)}, f32[64]{0:T(128)S(1)}) all-reduce(f32[28,64]{1,0:T(8,128)S(1)} %convolution_bitcast_fusion.3, f32[64]{0:T(128)S(1)} %get-tuple-element.141), channel_id=1, replica_groups=mesh['parts'=1,'data'=128] {'data'}, use_global_device_ids=true, to_apply=%region_2.2 | all-reduce | flops 1856 | bytes 14848 | tf_op jit(solution)/shard_map/while/body/eval_jaxpr/psum | solution.py:20
  2320.9 64.2 %all-reduce.2 = (f32[28,64]{1,0:T(8,128)S(1)}, f32[64]{0:T(128)S(1)}) all-reduce(f32[28,64]{1,0:T(8,128)S(1)} %convolution_bitcast_fusion.3, f32[64]{0:T(128)S(1)} %get-tuple-element.141), channel_id=1, replica_groups=mesh['parts'=1,'data'=128] {'data'}, use_global_device_ids=true, to_apply=%region_2.2 | all-reduce | flops 1856 | bytes 14848 | tf_op jit(solution)/shard_map/while/body/eval_jaxpr/psum | solution.py:20
  2389.7 62.8 %all-reduce.2 = (f32[28,64]{1,0:T(8,128)S(1)}, f32[64]{0:T(128)S(1)}) all-reduce(f32[28,64]{1,0:T(8,128)S(1)} %convolution_bitcast_fusion.3, f32[64]{0:T(128)S(1)} %get-tuple-element.141), channel_id=1, replica_groups=mesh['parts'=1,'data'=128] {'data'}, use_global_device_ids=true, to_apply=%region_2.2 | all-reduce | flops 1856 | bytes 14848 | tf_op jit(solution)/shard_map/while/body/eval_jaxpr/psum | solution.py:20
  2457.0 64.2 %all-reduce.2 = (f32[28,64]{1,0:T(8,128)S(1)}, f32[64]{0:T(128)S(1)}) all-reduce(f32[28,64]{1,0:T(8,128)S(1)} %convolution_bitcast_fusion.3, f32[64]{0:T(128)S(1)} %get-tuple-element.141), channel_id=1, replica_groups=mesh['parts'=1,'data'=128] {'data'}, use_global_device_ids=true, to_apply=%region_2.2 | all-reduce | flops 1856 | bytes 14848 | tf_op jit(solution)/shard_map/while/body/eval_jaxpr/psum | solution.py:20
  2525.8 62.8 %all-reduce.2 = (f32[28,64]{1,0:T(8,128)S(1)}, f32[64]{0:T(128)S(1)}) all-reduce(f32[28,64]{1,0:T(8,128)S(1)} %convolution_bitcast_fusion.3, f32[64]{0:T(128)S(1)} %get-tuple-element.141), channel_id=1, replica_groups=mesh['parts'=1,'data'=128] {'data'}, use_global_device_ids=true, to_apply=%region_2.2 | all-reduce | flops 1856 | bytes 14848 | tf_op jit(solution)/shard_map/while/body/eval_jaxpr/psum | solution.py:20
  2593.1 64.2 %all-reduce.2 = (f32[28,64]{1,0:T(8,128)S(1)}, f32[64]{0:T(128)S(1)}) all-reduce(f32[28,64]{1,0:T(8,128)S(1)} %convolution_bitcast_fusion.3, f32[64]{0:T(128)S(1)} %get-tuple-element.141), channel_id=1, replica_groups=mesh['parts'=1,'data'=128] {'data'}, use_global_device_ids=true, to_apply=%region_2.2 | all-reduce | flops 1856 | bytes 14848 | tf_op jit(solution)/shard_map/while/body/eval_jaxpr/psum | solution.py:20
  2661.9 62.8 %all-reduce.2 = (f32[28,64]{1,0:T(8,128)S(1)}, f32[64]{0:T(128)S(1)}) all-reduce(f32[28,64]{1,0:T(8,128)S(1)} %convolution_bitcast_fusion.3, f32[64]{0:T(128)S(1)} %get-tuple-element.141), channel_id=1, replica_groups=mesh['parts'=1,'data'=128] {'data'}, use_global_device_ids=true, to_apply=%region_2.2 | all-reduce | flops 1856 | bytes 14848 | tf_op jit(solution)/shard_map/while/body/eval_jaxpr/psum | solution.py:20
  2729.2 64.2 %all-reduce.2 = (f32[28,64]{1,0:T(8,128)S(1)}, f32[64]{0:T(128)S(1)}) all-reduce(f32[28,64]{1,0:T(8,128)S(1)} %convolution_bitcast_fusion.3, f32[64]{0:T(128)S(1)} %get-tuple-element.141), channel_id=1, replica_groups=mesh['parts'=1,'data'=128] {'data'}, use_global_device_ids=true, to_apply=%region_2.2 | all-reduce | flops 1856 | bytes 14848 | tf_op jit(solution)/shard_map/while/body/eval_jaxpr/psum | solution.py:20
  2798.0 62.8 %all-reduce.2 = (f32[28,64]{1,0:T(8,128)S(1)}, f32[64]{0:T(128)S(1)}) all-reduce(f32[28,64]{1,0:T(8,128)S(1)} %convolution_bitcast_fusion.3, f32[64]{0:T(128)S(1)} %get-tuple-element.141), channel_id=1, replica_groups=mesh['parts'=1,'data'=128] {'data'}, use_global_device_ids=true, to_apply=%region_2.2 | all-reduce | flops 1856 | bytes 14848 | tf_op jit(solution)/shard_map/while/body/eval_jaxpr/psum | solution.py:20
  2865.3 64.2 %all-reduce.2 = (f32[28,64]{1,0:T(8,128)S(1)}, f32[64]{0:T(128)S(1)}) all-reduce(f32[28,64]{1,0:T(8,128)S(1)} %convolution_bitcast_fusion.3, f32[64]{0:T(128)S(1)} %get-tuple-element.141), channel_id=1, replica_groups=mesh['parts'=1,'data'=128] {'data'}, use_global_device_ids=true, to_apply=%region_2.2 | all-reduce | flops 1856 | bytes 14848 | tf_op jit(solution)/shard_map/while/body/eval_jaxpr/psum | solution.py:20
  2934.1 62.8 %all-reduce.2 = (f32[28,64]{1,0:T(8,128)S(1)}, f32[64]{0:T(128)S(1)}) all-reduce(f32[28,64]{1,0:T(8,128)S(1)} %convolution_bitcast_fusion.3, f32[64]{0:T(128)S(1)} %get-tuple-element.141), channel_id=1, replica_groups=mesh['parts'=1,'data'=128] {'data'}, use_global_device_ids=true, to_apply=%region_2.2 | all-reduce | flops 1856 | bytes 14848 | tf_op jit(solution)/shard_map/while/body/eval_jaxpr/psum | solution.py:20
  3001.4 64.2 %all-reduce.2 = (f32[28,64]{1,0:T(8,128)S(1)}, f32[64]{0:T(128)S(1)}) all-reduce(f32[28,64]{1,0:T(8,128)S(1)} %convolution_bitcast_fusion.3, f32[64]{0:T(128)S(1)} %get-tuple-element.141), channel_id=1, replica_groups=mesh['parts'=1,'data'=128] {'data'}, use_global_device_ids=true, to_apply=%region_2.2 | all-reduce | flops 1856 | bytes 14848 | tf_op jit(solution)/shard_map/while/body/eval_jaxpr/psum | solution.py:20
  3070.1 62.8 %all-reduce.2 = (f32[28,64]{1,0:T(8,128)S(1)}, f32[64]{0:T(128)S(1)}) all-reduce(f32[28,64]{1,0:T(8,128)S(1)} %convolution_bitcast_fusion.3, f32[64]{0:T(128)S(1)} %get-tuple-element.141), channel_id=1, replica_groups=mesh['parts'=1,'data'=128] {'data'}, use_global_device_ids=true, to_apply=%region_2.2 | all-reduce | flops 1856 | bytes 14848 | tf_op jit(solution)/shard_map/while/body/eval_jaxpr/psum | solution.py:20
  3137.4 64.2 %all-reduce.2 = (f32[28,64]{1,0:T(8,128)S(1)}, f32[64]{0:T(128)S(1)}) all-reduce(f32[28,64]{1,0:T(8,128)S(1)} %convolution_bitcast_fusion.3, f32[64]{0:T(128)S(1)} %get-tuple-element.141), channel_id=1, replica_groups=mesh['parts'=1,'data'=128] {'data'}, use_global_device_ids=true, to_apply=%region_2.2 | all-reduce | flops 1856 | bytes 14848 | tf_op jit(solution)/shard_map/while/body/eval_jaxpr/psum | solution.py:20
  3206.2 62.8 %all-reduce.2 = (f32[28,64]{1,0:T(8,128)S(1)}, f32[64]{0:T(128)S(1)}) all-reduce(f32[28,64]{1,0:T(8,128)S(1)} %convolution_bitcast_fusion.3, f32[64]{0:T(128)S(1)} %get-tuple-element.141), channel_id=1, replica_groups=mesh['parts'=1,'data'=128] {'data'}, use_global_device_ids=true, to_apply=%region_2.2 | all-reduce | flops 1856 | bytes 14848 | tf_op jit(solution)/shard_map/while/body/eval_jaxpr/psum | solution.py:20
  3273.5 64.2 %all-reduce.2 = (f32[28,64]{1,0:T(8,128)S(1)}, f32[64]{0:T(128)S(1)}) all-reduce(f32[28,64]{1,0:T(8,128)S(1)} %convolution_bitcast_fusion.3, f32[64]{0:T(128)S(1)} %get-tuple-element.141), channel_id=1, replica_groups=mesh['parts'=1,'data'=128] {'data'}, use_global_device_ids=true, to_apply=%region_2.2 | all-reduce | flops 1856 | bytes 14848 | tf_op jit(solution)/shard_map/while/body/eval_jaxpr/psum | solution.py:20
  3342.3 62.8 %all-reduce.2 = (f32[28,64]{1,0:T(8,128)S(1)}, f32[64]{0:T(128)S(1)}) all-reduce(f32[28,64]{1,0:T(8,128)S(1)} %convolution_bitcast_fusion.3, f32[64]{0:T(128)S(1)} %get-tuple-element.141), channel_id=1, replica_groups=mesh['parts'=1,'data'=128] {'data'}, use_global_device_ids=true, to_apply=%region_2.2 | all-reduce | flops 1856 | bytes 14848 | tf_op jit(solution)/shard_map/while/body/eval_jaxpr/psum | solution.py:20
  3409.6 64.2 %all-reduce.2 = (f32[28,64]{1,0:T(8,128)S(1)}, f32[64]{0:T(128)S(1)}) all-reduce(f32[28,64]{1,0:T(8,128)S(1)} %convolution_bitcast_fusion.3, f32[64]{0:T(128)S(1)} %get-tuple-element.141), channel_id=1, replica_groups=mesh['parts'=1,'data'=128] {'data'}, use_global_device_ids=true, to_apply=%region_2.2 | all-reduce | flops 1856 | bytes 14848 | tf_op jit(solution)/shard_map/while/body/eval_jaxpr/psum | solution.py:20
  3478.4 62.8 %all-reduce.2 = (f32[28,64]{1,0:T(8,128)S(1)}, f32[64]{0:T(128)S(1)}) all-reduce(f32[28,64]{1,0:T(8,128)S(1)} %convolution_bitcast_fusion.3, f32[64]{0:T(128)S(1)} %get-tuple-element.141), channel_id=1, replica_groups=mesh['parts'=1,'data'=128] {'data'}, use_global_device_ids=true, to_apply=%region_2.2 | all-reduce | flops 1856 | bytes 14848 | tf_op jit(solution)/shard_map/while/body/eval_jaxpr/psum | solution.py:20
  3545.7 64.2 %all-reduce.2 = (f32[28,64]{1,0:T(8,128)S(1)}, f32[64]{0:T(128)S(1)}) all-reduce(f32[28,64]{1,0:T(8,128)S(1)} %convolution_bitcast_fusion.3, f32[64]{0:T(128)S(1)} %get-tuple-element.141), channel_id=1, replica_groups=mesh['parts'=1,'data'=128] {'data'}, use_global_device_ids=true, to_apply=%region_2.2 | all-reduce | flops 1856 | bytes 14848 | tf_op jit(solution)/shard_map/while/body/eval_jaxpr/psum | solution.py:20
  3614.5 62.8 %all-reduce.2 = (f32[28,64]{1,0:T(8,128)S(1)}, f32[64]{0:T(128)S(1)}) all-reduce(f32[28,64]{1,0:T(8,128)S(1)} %convolution_bitcast_fusion.3, f32[64]{0:T(128)S(1)} %get-tuple-element.141), channel_id=1, replica_groups=mesh['parts'=1,'data'=128] {'data'}, use_global_device_ids=true, to_apply=%region_2.2 | all-reduce | flops 1856 | bytes 14848 | tf_op jit(solution)/shard_map/while/body/eval_jaxpr/psum | solution.py:20
  3681.8 64.2 %all-reduce.2 = (f32[28,64]{1,0:T(8,128)S(1)}, f32[64]{0:T(128)S(1)}) all-reduce(f32[28,64]{1,0:T(8,128)S(1)} %convolution_bitcast_fusion.3, f32[64]{0:T(128)S(1)} %get-tuple-element.141), channel_id=1, replica_groups=mesh['parts'=1,'data'=128] {'data'}, use_global_device_ids=true, to_apply=%region_2.2 | all-reduce | flops 1856 | bytes 14848 | tf_op jit(solution)/shard_map/while/body/eval_jaxpr/psum | solution.py:20
  3750.6 62.8 %all-reduce.2 = (f32[28,64]{1,0:T(8,128)S(1)}, f32[64]{0:T(128)S(1)}) all-reduce(f32[28,64]{1,0:T(8,128)S(1)} %convolution_bitcast_fusion.3, f32[64]{0:T(128)S(1)} %get-tuple-element.141), channel_id=1, replica_groups=mesh['parts'=1,'data'=128] {'data'}, use_global_device_ids=true, to_apply=%region_2.2 | all-reduce | flops 1856 | bytes 14848 | tf_op jit(solution)/shard_map/while/body/eval_jaxpr/psum | solution.py:20
  3817.9 64.2 %all-reduce.2 = (f32[28,64]{1,0:T(8,128)S(1)}, f32[64]{0:T(128)S(1)}) all-reduce(f32[28,64]{1,0:T(8,128)S(1)} %convolution_bitcast_fusion.3, f32[64]{0:T(128)S(1)} %get-tuple-element.141), channel_id=1, replica_groups=mesh['parts'=1,'data'=128] {'data'}, use_global_device_ids=true, to_apply=%region_2.2 | all-reduce | flops 1856 | bytes 14848 | tf_op jit(solution)/shard_map/while/body/eval_jaxpr/psum | solution.py:20
  3954.0 64.2 %all-reduce.2 = (f32[28,64]{1,0:T(8,128)S(1)}, f32[64]{0:T(128)S(1)}) all-reduce(f32[28,64]{1,0:T(8,128)S(1)} %convolution_bitcast_fusion.3, f32[64]{0:T(128)S(1)} %get-tuple-element.141), channel_id=1, replica_groups=mesh['parts'=1,'data'=128] {'data'}, use_global_device_ids=true, to_apply=%region_2.2 | all-reduce | flops 1856 | bytes 14848 | tf_op jit(solution)/shard_map/while/body/eval_jaxpr/psum | solution.py:20
  4022.7 62.8 %all-reduce.2 = (f32[28,64]{1,0:T(8,128)S(1)}, f32[64]{0:T(128)S(1)}) all-reduce(f32[28,64]{1,0:T(8,128)S(1)} %convolution_bitcast_fusion.3, f32[64]{0:T(128)S(1)} %get-tuple-element.141), channel_id=1, replica_groups=mesh['parts'=1,'data'=128] {'data'}, use_global_device_ids=true, to_apply=%region_2.2 | all-reduce | flops 1856 | bytes 14848 | tf_op jit(solution)/shard_map/while/body/eval_jaxpr/psum | solution.py:20
  4090.0 64.2 %all-reduce.2 = (f32[28,64]{1,0:T(8,128)S(1)}, f32[64]{0:T(128)S(1)}) all-reduce(f32[28,64]{1,0:T(8,128)S(1)} %convolution_bitcast_fusion.3, f32[64]{0:T(128)S(1)} %get-tuple-element.141), channel_id=1, replica_groups=mesh['parts'=1,'data'=128] {'data'}, use_global_device_ids=true, to_apply=%region_2.2 | all-reduce | flops 1856 | bytes 14848 | tf_op jit(solution)/shard_map/while/body/eval_jaxpr/psum | solution.py:20
  4226.1 64.2 %all-reduce.2 = (f32[28,64]{1,0:T(8,128)S(1)}, f32[64]{0:T(128)S(1)}) all-reduce(f32[28,64]{1,0:T(8,128)S(1)} %convolution_bitcast_fusion.3, f32[64]{0:T(128)S(1)} %get-tuple-element.141), channel_id=1, replica_groups=mesh['parts'=1,'data'=128] {'data'}, use_global_device_ids=true, to_apply=%region_2.2 | all-reduce | flops 1856 | bytes 14848 | tf_op jit(solution)/shard_map/while/body/eval_jaxpr/psum | solution.py:20
  4294.9 62.8 %all-reduce.2 = (f32[28,64]{1,0:T(8,128)S(1)}, f32[64]{0:T(128)S(1)}) all-reduce(f32[28,64]{1,0:T(8,128)S(1)} %convolution_bitcast_fusion.3, f32[64]{0:T(128)S(1)} %get-tuple-element.141), channel_id=1, replica_groups=mesh['parts'=1,'data'=128] {'data'}, use_global_device_ids=true, to_apply=%region_2.2 | all-reduce | flops 1856 | bytes 14848 | tf_op jit(solution)/shard_map/while/body/eval_jaxpr/psum | solution.py:20
  4362.2 64.2 %all-reduce.2 = (f32[28,64]{1,0:T(8,128)S(1)}, f32[64]{0:T(128)S(1)}) all-reduce(f32[28,64]{1,0:T(8,128)S(1)} %convolution_bitcast_fusion.3, f32[64]{0:T(128)S(1)} %get-tuple-element.141), channel_id=1, replica_groups=mesh['parts'=1,'data'=128] {'data'}, use_global_device_ids=true, to_apply=%region_2.2 | all-reduce | flops 1856 | bytes 14848 | tf_op jit(solution)/shard_map/while/body/eval_jaxpr/psum | solution.py:20
  (463 shorter events, 420.6 us)
Async XLA Ops:
  2.1 70.9 %copy-start.2 = (f32[28,64]{1,0:T(8,128)S(1)}, f32[28,64]{1,0:T(8,128)}, u32[]{:S(2)}) copy-start(f32[28,64]{1,0:T(8,128)} %param.10) | copy-start | bytes 21508
  2.1 70.9 %copy-start.3 = (bf16[8192,28]{0,1:T(8,128)(2,1)S(1)}, bf16[8192,28]{0,1:T(8,128)(2,1)}, u32[]{:S(2)}) copy-start(bf16[8192,28]{0,1:T(8,128)(2,1)} %param.7) | copy-start | bytes 1376260
  4427.8 0.6 copy-start
  4427.8 0.6 copy-start.1
where the time goes:
time: 4440 us; the launch traced here: 4430 us
  blocking collectives  4130 us (93%)
  matrix products  161 us (4%)
  local copies, waits for them, and re-layouts  84.5 us (2%)
  other arithmetic  49.1 us (1%)
    psum x65, blocking collectives, gradient_at(): gradient = lax.psum(grad_part, 'data') - positions / PRIOR_VAR  4130 us
    dot_general x64, matrix products, gradient_at(): jnp.dot(feat_rows, positions.astype(jnp.bfloat16), preferred_element_type...  107 us

commit v1 on v0

v1 whole, which is shorter than its diff:
```python
import itertools

import jax
import jax.numpy as jnp
from jax import lax
from jax.experimental import pallas as pl
from jax.experimental.pallas import tpu as pltpu
from jax.sharding import PartitionSpec as P

PRIOR_VAR = 4.0
FEATURES = 28
STEPS = 64
CHAINS = 64
HALF = 32
ROWS = 8192
PACK = 8
PROWS = ROWS // PACK
CHUNK = 256
GROUP = 64
MESSAGE = 7
OFFSETS = list(itertools.product(range(4), repeat=3))


def hops(offset):
    return sum(min(step, 4 - step) for step in offset)


FAR_FIRST = sorted(range(1, 64), key=lambda k: -hops(OFFSETS[k]))


def ring_sum(values):
    if len(values) == 1:
        return values[0]
    quarter = len(values) // 4
    part = [ring_sum(values[i * quarter:(i + 1) * quarter]) for i in range(4)]
    return (part[0] + part[2]) + (part[1] + part[3])


def chain_kernel(rows_ref, pos_ref, mom_ref, eps_ref, out_ref,
                 packed, packed_t, weights, resid, outgoing, incoming, loss_rows, kin_rows,
                 energy_out, energy_in, final,
                 send_sem, recv_sem, esend_sem, erecv_sem, pair_send, pair_recv):
    index = lax.axis_index("data")
    core = index % 2
    x, y, z = (index // 2) % 4, (index // 8) % 4, index // 32
    partner = (0, index + 1 - 2 * core)

    def peer(offset):
        return (0, ((((z + offset[0]) % 4) * 4 + (y + offset[1]) % 4) * 4 + (x + offset[2]) % 4) * 2 + core)

    lane = lax.broadcasted_iota(jnp.int32, (8, 128), 1) // HALF
    lane16 = lax.broadcasted_iota(jnp.int32, (16, 128), 1) // HALF
    real_row = lax.broadcasted_iota(jnp.int32, (8, 128), 0) < MESSAGE

    def pair_copy(ref, src, dst, slot):
        return pltpu.make_async_remote_copy(src_ref=ref.at[src], dst_ref=ref.at[dst], send_sem=pair_send.at[slot], recv_sem=pair_recv.at[slot], device_id=partner, device_id_type=pl.DeviceIdType.MESH)

    column = lax.broadcasted_iota(jnp.int32, (FEATURES, 256), 1)
    feature = lax.broadcasted_iota(jnp.int32, (FEATURES, 256), 0)
    wanted = ((column % 32) // 8) * 7 + column % 8
    place = (feature == wanted) & (column % 8 < 7)
    for r in range(PROWS // CHUNK):
        acc = jnp.zeros((CHUNK, 256), jnp.float32)
        for g in range(PACK):
            place_g = jnp.where(place & (column // 32 == g), 1.0, 0.0).astype(jnp.bfloat16)
            acc = acc + jnp.dot(rows_ref[g * PROWS + r * CHUNK:g * PROWS + (r + 1) * CHUNK, :], place_g, preferred_element_type=jnp.float32)
        packed[0, r * CHUNK:(r + 1) * CHUNK, :] = acc.astype(jnp.bfloat16)
        packed_t[0, :, r * CHUNK:(r + 1) * CHUNK] = acc.T.astype(jnp.bfloat16)
    pair_copy(packed, 0, 1, 0).start()
    pair_copy(packed_t, 0, 1, 1).start()
    weights[...] = jnp.zeros_like(weights)
    pair_copy(packed, 0, 1, 0).wait()
    pair_copy(packed_t, 0, 1, 1).wait()

    def lane_total(row):
        row = row + pltpu.roll(row, 64, 1)
        return row + pltpu.roll(row, 32, 1)

    def evaluate(positions, parity, loss_index, last):
        half = positions.astype(jnp.bfloat16).astype(jnp.float32) * 0.5
        turned = [half] + [pltpu.roll(half, 32 * k, 1) for k in range(1, 4)]
        for j in range(4):
            for p in range(2):
                block = jnp.concatenate([turned[(j - 2 * p) % 4], turned[(j - 2 * p - 1) % 4]], axis=0)
                block = jnp.where(lane16 == j, block, 0.0).astype(jnp.bfloat16)
                for h in range(2):
                    row = 32 * (4 * h + j) + 16 * p
                    weights[row:row + 16, 128 * h:128 * (h + 1)] = block
        linear = jnp.zeros((8, 256), jnp.float32)
        logs = jnp.zeros((8, 256), jnp.float32)
        grads = [None, None]
        product = None
        count = 0
        for b in range(2):
            for r in range(PROWS // CHUNK):
                span = slice(r * CHUNK, (r + 1) * CHUNK)
                logit = jnp.dot(packed[b, span, :], weights[...], preferred_element_type=jnp.float32)
                bent = jnp.tanh(logit)
                part = (1.0 + bent).astype(jnp.bfloat16)
                for h in range(2):
                    cols = slice(128 * h, 128 * (h + 1))
                    piece = jnp.dot(packed_t[b, cols, span], part[:, cols], preferred_element_type=jnp.float32)
                    grads[h] = piece if grads[h] is None else grads[h] + piece
                factor = 1.0 + jnp.abs(bent)
                positive = jnp.maximum(logit, 0.0)
                for i in range(CHUNK // 8):
                    rows8 = slice(8 * i, 8 * i + 8)
                    linear = linear + positive[rows8]
                    product = factor[rows8] if product is None else product * factor[rows8]
                    count += 1
                    if count == GROUP:
                        logs = logs + jnp.log(product * 2.0 ** -GROUP)
                        product, count = None, 0
        blocks = []
        for q in range(4):
            total = None
            for h in range(2):
                pick = grads[h][8 * q:8 * q + 8]
                for j in range(1, 4):
                    pick = jnp.where(lane == j, grads[h][32 * j + 8 * q:32 * j + 8 * q + 8], pick)
                total = pick if total is None else total + pick
            blocks.append(total)
        message = None
        for k in range(4):
            turn = blocks[-k % 4]
            for j in range(1, 4):
                turn = jnp.where(lane == j, blocks[(j - k) % 4], turn)
            message = turn if k == 0 else message + pltpu.roll(turn, 128 - 32 * k, 1)
        outgoing[parity] = message

        def gradient_copy(k):
            return pltpu.make_async_remote_copy(src_ref=outgoing.at[parity, 0:MESSAGE], dst_ref=incoming.at[parity, k, 0:MESSAGE], send_sem=send_sem.at[parity], recv_sem=recv_sem.at[parity, k // 16], device_id=peer(OFFSETS[k]), device_id_type=pl.DeviceIdType.MESH)

        for k in FAR_FIRST:
            gradient_copy(k).start()

        loss = 2.0 * linear - logs
        loss = jnp.sum(loss[:, :128] + loss[:, 128:], axis=0, keepdims=True)
        loss_rows[pl.ds(loss_index + 7, 1), :] = lane_total(loss)

        def energy_copy(k):
            return pltpu.make_async_remote_copy(src_ref=energy_out, dst_ref=energy_in.at[k], send_sem=esend_sem.at[0], recv_sem=erecv_sem.at[k // 16], device_id=peer(OFFSETS[k]), device_id_type=pl.DeviceIdType.MESH)

        if last:
            own = loss_rows[8:24, :]
            for q in range(1, 4):
                own = jnp.where(lane16 == q, loss_rows[8 + 16 * q:24 + 16 * q, :], own)
            energy_out[...] = own
            for k in FAR_FIRST:
                energy_copy(k).start()

        def wait_planes(buffer, rows, sems):
            for plane in (0, 1, 3, 2):
                low = max(16 * plane, 1)
                ref = buffer.at[low:16 * plane + 16, 0:rows] if rows else buffer.at[low:16 * plane + 16]
                pltpu.make_async_copy(ref, ref, sems.at[plane]).wait()

        wait_planes(incoming.at[parity], MESSAGE, recv_sem.at[parity])
        total = ring_sum([message if k == 0 else incoming[parity, k] for k in range(64)])
        sent = incoming.at[parity, 1:64, 0:MESSAGE]
        pltpu.make_async_copy(sent, sent, send_sem.at[parity]).wait()
        gradient = jnp.where(real_row, -0.5 * total - positions / PRIOR_VAR, 0.0)
        if not last:
            return gradient
        wait_planes(energy_in, 0, erecv_sem)
        losses = ring_sum([energy_out[...] if k == 0 else energy_in[k] for k in range(64)])
        sent = energy_in.at[1:64]
        pltpu.make_async_copy(sent, sent, esend_sem.at[0]).wait()
        return gradient, losses

    def kinetic(positions, momentum, row):
        value = positions * positions / (2.0 * PRIOR_VAR) + 0.5 * (momentum * momentum)
        kin_rows[pl.ds(row + 7, 1), :] = lane_total(jnp.sum(value, axis=0, keepdims=True))

    def leap(number, parity, state, last=False):
        positions, momentum, gradient = state
        step_size = eps_ref[core, pl.ds(number, 1), :]
        momentum_half = momentum + 0.5 * step_size * gradient
        moved = positions + step_size * momentum_half
        result = evaluate(moved, parity, number, last)
        kinetic(positions, momentum, jnp.maximum(number - 1, 0))
        gradient = result[0] if last else result
        momentum = momentum_half + 0.5 * step_size * gradient
        if not last:
            return moved, momentum, gradient
        kinetic(moved, momentum, number)
        return moved, momentum, result[1]

    def two_leaps(i, state):
        return leap(2 * i + 1, 1, leap(2 * i, 0, state))

    state = (pos_ref[core], mom_ref[core], jnp.zeros((8, 128), jnp.float32))
    state = lax.fori_loop(0, STEPS // 2, two_leaps, state)
    positions, momentum, energy = leap(STEPS, 0, state, last=True)

    local = kin_rows[8:24, :]
    for q in range(1, 4):
        local = jnp.where(lane16 == q, kin_rows[8 + 16 * q:24 + 16 * q, :], local)
    final[core, 0:8, :] = positions
    final[core, 8:16, :] = momentum
    final[core, 16:32, :] = energy + local
    pair_copy(final, core, core, 2).start()
    pair_copy(final, core, core, 2).wait()
    out_ref[...] = final[...]


def to_lanes(array):
    split = array.reshape(4, 7, 2, HALF).transpose(2, 1, 0, 3).reshape(2, 7, 128)
    return jnp.pad(split, ((0, 0), (0, 1), (0, 0)))


def from_lanes(array):
    return array[:, :7].reshape(2, 7, 4, HALF).transpose(2, 1, 0, 3).reshape(FEATURES, CHAINS)


def solution(mesh):
    row_spec = P("data", None)
    chain_spec = P(None, "parts")

    def local_chains(feat_rows, labels, pos_init, mom_init, step_sizes):
        signed = feat_rows * (1 - 2 * labels).astype(jnp.bfloat16)[:, None]
        eps = jnp.pad(step_sizes, ((1, 7), (0, 0))).reshape(72, 2, 1, HALF)
        eps = jnp.broadcast_to(eps, (72, 2, 4, HALF)).transpose(1, 0, 2, 3).reshape(2, 72, 128)
        vmem = pl.BlockSpec(memory_space=pltpu.VMEM)
        final = pl.pallas_call(
            chain_kernel,
            out_shape=jax.ShapeDtypeStruct((2, 32, 128), jnp.float32),
            in_specs=[vmem] * 4,
            out_specs=vmem,
            scratch_shapes=[
                pltpu.VMEM((2, PROWS, 256), jnp.bfloat16),
                pltpu.VMEM((2, 256, PROWS), jnp.bfloat16),
                pltpu.VMEM((256, 256), jnp.bfloat16),
                pltpu.VMEM((16, 128), jnp.bfloat16),
                pltpu.VMEM((2, 8, 128), jnp.float32),
                pltpu.VMEM((2, 64, 8, 128), jnp.float32),
                pltpu.VMEM((80, 128), jnp.float32),
                pltpu.VMEM((80, 128), jnp.float32),
                pltpu.VMEM((16, 128), jnp.float32),
                pltpu.VMEM((64, 16, 128), jnp.float32),
                pltpu.VMEM((2, 32, 128), jnp.float32),
                pltpu.SemaphoreType.DMA((2,)),
                pltpu.SemaphoreType.DMA((2, 4)),
                pltpu.SemaphoreType.DMA((1,)),
                pltpu.SemaphoreType.DMA((4,)),
                pltpu.SemaphoreType.DMA((3,)),
                pltpu.SemaphoreType.DMA((3,)),
            ],
            compiler_params=pltpu.CompilerParams(has_side_effects=True),
            name="chains",
        )(signed, to_lanes(pos_init), to_lanes(mom_init), eps)
        energies = final[:, 16:32].reshape(2, 16, 4, HALF).transpose(2, 1, 0, 3).reshape(STEPS, CHAINS)
        return from_lanes(final[:, 0:8]), from_lanes(final[:, 8:16]), energies

    return jax.shard_map(local_chains, mesh=mesh, in_specs=(row_spec, P("data"), chain_spec, chain_spec, chain_spec), out_specs=(chain_spec, chain_spec, chain_spec), check_vma=False)
```

time: 4440 us -> 532 us (0.12)
  blocking collectives: 4130 us -> 0 us
  Pallas kernels: 0 us -> 517 us
  matrix products: 161 us -> 0 us
  local copies, waits for them, and re-layouts: 84.5 us -> 10.5 us
  other arithmetic: 49.1 us -> 3.04 us
    psum x65 -> x0, blocking collectives: 4130 us -> none  [gradient_at(): gradient = lax.psum(grad_part, 'data') - positions / PRIOR_VAR]
    pallas_call x0 -> x1, Pallas kernels: none -> 517 us  [local_chains(): pl.pallas_call(chain_kernel, out_shape=jax.ShapeDtypeStruct((2, 32, 128),...]
    dot_general x129 -> x0, matrix products: 161 us -> none  [the longest x64 107 us: gradient_at(): jnp.dot(feat_rows, positions.astype(jnp.bfloat16), preferred_element_type...]
    dynamic_update_slice x64 -> x0, local copies, waits for them, and re-layouts: 83.1 us -> none  [local_chains(): lax.scan(leap_step, (pos_init, mom_init, grad_init), step_sizes)]
where the time goes in v1:
time: 532 us; the launch traced here: 531 us
  Pallas kernels  517 us (97%)
  local copies, waits for them, and re-layouts  10.5 us (2%)
    pallas_call x1, Pallas kernels, local_chains(): pl.pallas_call(chain_kernel, out_shape=jax.ShapeDtypeStruct((2, 32, 128),...  517 us

profile of v1, /device:TPU:1, one launch (start us, length us, event | category | flops | bytes accessed | tf_op | source)
XLA Modules:
  0.0 531.2 jit_solution(15338326375127043507)
XLA Ops:
  0.6 0.8 subtract_convert_fusion
  1.4 0.8 reshape.42
  2.2 0.1 reshape.43
  2.3 0.6 pad.11.pos_ref
  2.9 0.8 reshape.44
  3.7 0.1 reshape.45
  3.8 0.6 pad.12.mom_ref
  4.4 0.8 copy.43
  5.3 0.1 pad.13
  5.4 0.7 copy.44.eps_ref
  6.1 2.0 copy.37
  8.1 2.3 broadcast_multiply_fusion.rows_ref
  10.3 516.9 %chains.1 = f32[2,32,128]{2,1,0:T(8,128)} custom-call(bf16[8192,28]{1,0:T(8,128)(2,1)} %broadcast_multiply_fusion.rows_ref, f32[2,8,128]{2,1,0:T(8,128)} %pad.11.pos_ref, f32[2,8,128]{2,1,0:T(8,128)} %pad.12.mom_ref, f32[2,72,128]{2,1,0:T(8,128)} %copy.44.eps_ref), custom_call_target="tpu_custom_call" | custom-call | tf_op jit(solution)/shard_map/chains/pallas_call | solution.py:225
  527.2 0.7 slice.15
  528.0 0.7 fusion
  528.7 0.1 reshape.47
  528.8 0.7 reshape.48
  529.5 0.1 reshape.49
  529.6 0.7 reshape.50
  530.3 0.1 reshape.51
  530.4 0.1 copy.49
  530.4 0.7 reshape.52
  (9 shorter events, 0.1 us)
